TPU v7x, 128 devices: a whole 4x4x4 slice. The times are simulated.
128 devices in a mesh: comp: 8 (over x_lo, y), dom: 16 (over z, x_hi, core).
Axes of the slice: x: 4 (x_hi: 2, x_lo: 2; x = x_hi * 2 + x_lo), y: 4, z: 4, core: 2. Of those that a mesh axis runs over, the one named last changes fastest.
Arguments:
- densities: float32 [8, 6144, 2048], P('comp', 'dom'), may hold values from -6 to 6
- levels: int32 [8, 2], P('comp'), may hold values from 0 to 3
- coeffs: int32 [8], P('comp'), may hold values from -1 to 1, as said below
Outputs:
- result: float32 [8, 6144, 2048], P('comp', 'dom')
Inputs may be any that keep to these rules, and one draw needn't show every extreme that they name: `coeffs`: each coefficient is -1 or 1; both values occur.
All inputs are finite; a program needn't handle non-finite values.
Results may differ from a plain program's by a relative error of at most 0.0001.
Values sent between devices are 32-bit elements; how exact they have to be, the bound alone decides.
A program may use at most 64 MiB of HBM per device.

v0:
```python
import functools

import jax
import jax.numpy as jnp
import numpy as np
from jax import lax
from jax.experimental import pallas as pl
from jax.experimental.pallas import tpu as pltpu
from jax.sharding import PartitionSpec as P

MX = 2048
MV = 256
PRE = 8
POST = 2
NV = 2048
ROWS = 384
NX = 6144
LANES = 128
TILES = NV // LANES
HALO = 16
LEAD = 24
PLANE_ROWS = 432
WIDE = 400
NCH = 4
KC = MX // NCH
KQ = KC // 4
MESH = pl.DeviceIdType.MESH
F32 = jnp.float32
BF16 = jnp.bfloat16

TWO_PI_HI = float(np.float32(6.28125))
TWO_PI_LO = float(np.float32(2.0 * np.pi - 6.28125))
INV_TWO_PI = float(np.float32(1.0 / (2.0 * np.pi)))


def sine_terms():
    count = 6
    nodes = np.cos(np.pi * (np.arange(64) + 0.5) / 128)
    r = np.pi * nodes
    u = r * r
    basis = np.stack([u**i for i in range(count)], axis=1)
    target = np.sqrt(2.0) * np.sin(r / 2) / r
    terms, *_ = np.linalg.lstsq(basis * r[:, None], target * r, rcond=None)
    return [float(np.float32(t)) for t in terms]


SINE_TERMS = sine_terms()


def cosine(phase):
    turns = jnp.round(phase * INV_TWO_PI)
    r = (phase - turns * TWO_PI_HI) - turns * TWO_PI_LO
    u = r * r
    s = jnp.full_like(u, SINE_TERMS[-1])
    for term in SINE_TERMS[-2::-1]:
        s = s * u + term
    s = s * r
    return 1.0 - s * s


def split(x):
    hi = x.astype(BF16)
    return hi, (x - hi.astype(F32)).astype(BF16)


def dot3(a_hi, a_lo, b_hi, b_lo, dims):
    def dot(a, b):
        return lax.dot_general(a, b, (dims, ((), ())), preferred_element_type=F32)

    return dot(a_hi, b_hi) + dot(a_hi, b_lo) + dot(a_lo, b_hi)


NN = ((1,), (0,))
NT = ((1,), (1,))


def kernel(
    lev_ref,
    coef_ref,
    dens_ref,
    out_ref,
    fa,
    fb,
    al_ref,
    be_ref,
    bx_h,
    bx_l,
    bv_h,
    bv_l,
    red_h,
    red_l,
    part,
    core_in,
    core_sum,
    z1_in,
    z1_sum,
    z2_in,
    block,
    plane_in,
    back_out,
    upd,
    corr,
    coef_own,
    coef_all,
    in_sem,
    out_sem,
    halo_send,
    halo_recv,
    coef_send,
    coef_recv,
    core_send,
    core_recv,
    z1_send,
    z1_recv,
    z2_send,
    z2_recv,
    plane_send,
    plane_recv,
    back_send,
    back_recv,
    g2_send,
    g2_recv,
    g1_send,
    g1_recv,
    gc_send,
    gc_recv,
):
    c = lax.axis_index("comp")
    d = lax.axis_index("dom")
    z = d // 4
    xh = (d // 2) % 2
    core = d % 2
    p = c * 2 + xh
    nxt = (d + 1) % 16
    prv = (d + 15) % 16
    peer = d + 1 - 2 * core
    za = (z + 1 - 2 * (z % 2)) * 4 + d % 4
    zb = (3 - z) * 4 + d % 4
    s1 = (z % 2 + z // 2) % 2
    s2 = z // 2
    t1 = z // 2
    t2 = s1

    def dom_id(dom):
        return {"comp": c, "dom": dom}

    def plane_id(q):
        return {"comp": q // 2, "dom": z * 4 + (q % 2) * 2 + core}

    barrier = pltpu.get_barrier_semaphore()
    for dom in (nxt, prv, peer, za, zb):
        pl.semaphore_signal(barrier, inc=1, device_id=dom_id(dom), device_id_type=MESH)
    for o in range(1, 16):
        q = (p + o) % 16
        pl.semaphore_signal(barrier, inc=1, device_id=plane_id(q), device_id_type=MESH)

    def load(t):
        return pltpu.make_async_copy(
            dens_ref.at[0, :, pl.ds(t * LANES, LANES)],
            fa.at[t, pl.ds(LEAD, ROWS), :],
            in_sem.at[t],
        )

    for t in range(TILES):
        load(t).start()

    lev_x = lev_ref[0, 0]
    lev_v = lev_ref[0, 1]
    courant = 0.3 + lev_x.astype(F32) / 15.0
    diffusion = 0.1 + lev_v.astype(F32) / 30.0
    coef_own[...] = jnp.full((8, LANES), coef_ref[0].astype(F32), F32)
    coef_all[c] = coef_own[...]

    def power(level):
        return jnp.where(level == 0, 8.0, jnp.where(level == 1, 4.0, jnp.where(level == 2, 2.0, 1.0))).astype(F32)

    lane = lax.broadcasted_iota(jnp.int32, (16, LANES), 1)
    row16 = lax.broadcasted_iota(jnp.int32, (16, LANES), 0)

    def velocity_basis(i, _):
        mode = (row16 + i * 16).astype(F32)
        r0 = pl.multiple_of(i * 16, 16)
        for t in range(TILES):
            cell = (lane + t * LANES).astype(F32)
            phase = ((np.float32(np.pi) * (cell + 0.5)) * mode) * np.float32(1.0 / NV)
            hi, lo = split(cosine(phase))
            bv_h[pl.ds(r0, 16), t * LANES : (t + 1) * LANES] = hi
            bv_l[pl.ds(r0, 16), t * LANES : (t + 1) * LANES] = lo
        return 0

    lax.fori_loop(0, MV // 16, velocity_basis, 0)

    for t in range(TILES):
        load(t).wait()
    pl.semaphore_wait(barrier, 20)

    halo_up = pltpu.make_async_remote_copy(
        src_ref=fa.at[:, pl.ds(LEAD, HALO), :],
        dst_ref=fa.at[:, pl.ds(LEAD + ROWS, HALO), :],
        send_sem=halo_send.at[0],
        recv_sem=halo_recv.at[0],
        device_id=dom_id(prv),
        device_id_type=MESH,
    )
    halo_down = pltpu.make_async_remote_copy(
        src_ref=fa.at[:, pl.ds(LEAD + ROWS - HALO, HALO), :],
        dst_ref=fa.at[:, pl.ds(LEAD - HALO, HALO), :],
        send_sem=halo_send.at[1],
        recv_sem=halo_recv.at[1],
        device_id=dom_id(nxt),
        device_id_type=MESH,
    )
    halo_up.start()
    halo_down.start()

    def coef_copy(o):
        return pltpu.make_async_remote_copy(
            src_ref=coef_own,
            dst_ref=coef_all.at[c],
            send_sem=coef_send.at[o],
            recv_sem=coef_recv.at[o],
            device_id={"comp": (c + o) % 8, "dom": d},
            device_id_type=MESH,
        )

    for o in range(1, 8):
        coef_copy(o).start()

    def space_basis(i, _):
        local = row16 + i * 16
        local = jnp.where(local >= ROWS + 8, local - WIDE, local)
        cell = local + d * ROWS
        cell = jnp.where(cell < 0, cell + NX, cell)
        cell = jnp.where(cell >= NX, cell - NX, cell)
        angle = np.float32(np.pi) * (cell.astype(F32) + 0.5)
        r0 = pl.multiple_of(i * 16, 16)
        for t in range(TILES):
            mode = (lane + t * LANES).astype(F32)
            phase = (angle * mode) * np.float32(1.0 / NX)
            hi, lo = split(cosine(phase))
            bx_h[pl.ds(r0, 16), t * LANES : (t + 1) * LANES] = hi
            bx_l[pl.ds(r0, 16), t * LANES : (t + 1) * LANES] = lo
        return 0

    lax.fori_loop(0, WIDE // 16, space_basis, 0)

    lane8 = lax.broadcasted_iota(jnp.int32, (8, LANES), 1)

    def set_rates(active):
        for t in range(TILES):
            cell = (lane8 + t * LANES).astype(F32)
            speed = jnp.abs(-1.0 + (2.0 * cell + 1.0) / NV) * courant
            al_ref[t] = 1.0 - active * (2.0 * diffusion + speed)
            be_ref[t] = active * speed
        return active * diffusion

    first_lane = lane == 0
    last_lane = lane == LANES - 1

    def step(src, dst, start, count, rate):
        def rows(i, _):
            r = start + i * 16
            r8 = pl.multiple_of(r, 8)
            f = [src[t, pl.ds(r8, 16), :] for t in range(TILES)]
            rl = [pltpu.roll(x, 1, 1) for x in f]
            rr = [pltpu.roll(x, LANES - 1, 1) for x in f]
            for t in range(TILES):
                left = jnp.where(first_lane, rl[t - 1] if t > 0 else f[0], rl[t])
                right = jnp.where(last_lane, rr[t + 1] if t < TILES - 1 else f[t], rr[t])
                shifted = src[t, pl.ds(r + 1 if t < TILES // 2 else r - 1, 16), :]
                al = jnp.concatenate([al_ref[t]] * 2, axis=0)
                be = jnp.concatenate([be_ref[t]] * 2, axis=0)
                dst[t, pl.ds(r8, 16), :] = al * f[t] + be * shifted + rate * (left + right)
            return 0

        lax.fori_loop(0, count // 16, rows, 0)

    rate = set_rates(jnp.float32(1.0))
    halo_up.wait_recv()
    halo_down.wait_recv()
    halo_up.wait_send()
    halo_down.wait_send()
    src, dst = fa, fb
    for s in range(PRE):
        if s >= PRE - 3:
            rate = set_rates(jnp.where(lev_x > s - (PRE - 3), 1.0, 0.0).astype(F32))
        if s == 0:
            step(src, dst, LEAD - HALO, ROWS + 2 * HALO, rate)
        else:
            step(src, dst, LEAD - 8, WIDE, rate)
        src, dst = dst, src

    reduced = jnp.zeros((ROWS, MV), F32)
    for kt in range(TILES // 2):
        block_f = jnp.concatenate([fa[2 * kt, LEAD : LEAD + ROWS, :], fa[2 * kt + 1, LEAD : LEAD + ROWS, :]], axis=1)
        a_hi, a_lo = split(block_f)
        cols = slice(kt * 256, (kt + 1) * 256)
        reduced = reduced + dot3(a_hi, a_lo, bv_h[:, cols], bv_l[:, cols], NT)
    hi, lo = split(reduced.T)
    red_h[...] = hi
    red_l[...] = lo

    def rows_of(base, size):
        return pl.ds(pl.multiple_of(base, size), size)

    def copy(src_ref, dst_ref, send, recv, dev):
        return pltpu.make_async_remote_copy(
            src_ref=src_ref, dst_ref=dst_ref, send_sem=send, recv_sem=recv, device_id=dev, device_id_type=MESH
        )

    def cols_of(k):
        return slice(k * KC, (k + 1) * KC)

    def core_copy(k):
        return copy(
            part.at[rows_of((1 - core) * 128, 128), pl.ds(k * KC, KC)],
            core_in.at[k],
            core_send.at[k],
            core_recv.at[k],
            dom_id(peer),
        )

    def z1_copies(k):
        return (
            copy(
                core_sum.at[k, rows_of((1 - s1) * 32, 32), :],
                z1_in.at[k, 0],
                z1_send.at[k, 0],
                z1_recv.at[k, 0],
                dom_id(za),
            ),
            copy(
                core_sum.at[k, rows_of(64 + (1 - t1) * 32, 32), :],
                z1_in.at[k, 1],
                z1_send.at[k, 1],
                z1_recv.at[k, 1],
                dom_id(zb),
            ),
        )

    def z2_copies(k):
        return (
            copy(
                z1_sum.at[k, 0, rows_of((1 - s2) * 16, 16), :],
                z2_in.at[k, 0],
                z2_send.at[k, 0],
                z2_recv.at[k, 0],
                dom_id(zb),
            ),
            copy(
                z1_sum.at[k, 1, rows_of((1 - t2) * 16, 16), :],
                z2_in.at[k, 1],
                z2_send.at[k, 1],
                z2_recv.at[k, 1],
                dom_id(za),
            ),
        )

    row_1 = core * 128 + s1 * 32 + s2 * 16
    row_2 = core * 128 + 64 + t1 * 32 + t2 * 16

    def plane_copy(k, o):
        q = (p + o) % 16
        return copy(
            block.at[k, rows_of((q // 4) * 8, 8), pl.ds(pl.multiple_of((q % 4) * KQ, KQ), KQ)],
            plane_in.at[k, o],
            plane_send.at[k, o],
            plane_recv.at[k, o],
            plane_id(q),
        )

    my_tile = p // 4
    my_row = jnp.where(my_tile < 2, row_1 + my_tile * 8, row_2 + (my_tile - 2) * 8)
    del my_row
    half = my_tile // 2
    own_row = row_1 + half * (row_2 - row_1) + (my_tile % 2) * 8
    own_lane = (p % 4) * KQ

    def own_tile(k):
        return (rows_of(own_row, 8), pl.ds(pl.multiple_of(k * KC + own_lane, KQ), KQ))

    def back_copy(k, o):
        q = (p + o) % 16
        return copy(
            back_out.at[k, q // 2],
            upd.at[own_tile(k)],
            back_send.at[k, o],
            back_recv.at[k, o],
            plane_id(q),
        )

    def back_wait(k, o):
        q = (p + 16 - o) % 16
        tile = q // 4
        row = row_1 + (tile // 2) * (row_2 - row_1) + (tile % 2) * 8
        dst = upd.at[rows_of(row, 8), pl.ds(pl.multiple_of(k * KC + (q % 4) * KQ, KQ), KQ)]
        copy(back_out.at[k, 0], dst, back_send.at[k, o], back_recv.at[k, o], plane_id(q)).wait_recv()

    def g2_copies(k):
        a = upd.at[rows_of(row_1, 16), pl.ds(k * KC, KC)]
        b = upd.at[rows_of(row_2, 16), pl.ds(k * KC, KC)]
        return (
            copy(a, a, g2_send.at[k, 0], g2_recv.at[k, 0], dom_id(zb)),
            copy(b, b, g2_send.at[k, 1], g2_recv.at[k, 1], dom_id(za)),
        )

    def g2_waits(k):
        a = upd.at[rows_of(core * 128 + s1 * 32 + (1 - s2) * 16, 16), pl.ds(k * KC, KC)]
        b = upd.at[rows_of(core * 128 + 64 + t1 * 32 + (1 - t2) * 16, 16), pl.ds(k * KC, KC)]
        copy(a, a, g2_send.at[k, 0], g2_recv.at[k, 0], dom_id(zb)).wait_recv()
        copy(b, b, g2_send.at[k, 1], g2_recv.at[k, 1], dom_id(za)).wait_recv()

    def g1_copies(k):
        a = upd.at[rows_of(core * 128 + s1 * 32, 32), pl.ds(k * KC, KC)]
        b = upd.at[rows_of(core * 128 + 64 + t1 * 32, 32), pl.ds(k * KC, KC)]
        return (
            copy(a, a, g1_send.at[k, 0], g1_recv.at[k, 0], dom_id(za)),
            copy(b, b, g1_send.at[k, 1], g1_recv.at[k, 1], dom_id(zb)),
        )

    def g1_waits(k):
        a = upd.at[rows_of(core * 128 + (1 - s1) * 32, 32), pl.ds(k * KC, KC)]
        b = upd.at[rows_of(core * 128 + 64 + (1 - t1) * 32, 32), pl.ds(k * KC, KC)]
        copy(a, a, g1_send.at[k, 0], g1_recv.at[k, 0], dom_id(za)).wait_recv()
        copy(b, b, g1_send.at[k, 1], g1_recv.at[k, 1], dom_id(zb)).wait_recv()

    def gc_copy(k):
        a = upd.at[rows_of(core * 128, 128), pl.ds(k * KC, KC)]
        return copy(a, a, gc_send.at[k], gc_recv.at[k], dom_id(peer))

    def gc_wait(k):
        a = upd.at[rows_of((1 - core) * 128, 128), pl.ds(k * KC, KC)]
        copy(a, a, gc_send.at[k], gc_recv.at[k], dom_id(peer)).wait_recv()

    fac_x = power(lev_x)
    fac_v = power(lev_v)

    def stage_project(k):
        part[:, cols_of(k)] = dot3(red_h[...], red_l[...], bx_h[0:ROWS, cols_of(k)], bx_l[0:ROWS, cols_of(k)], NN)
        core_copy(k).start()

    def stage_core(k):
        core_copy(k).wait_recv()
        core_sum[k] = part[rows_of(core * 128, 128), cols_of(k)] + core_in[k]
        for cp in z1_copies(k):
            cp.start()

    def stage_z1(k):
        for cp in z1_copies(k):
            cp.wait_recv()
        z1_sum[k, 0] = core_sum[k, rows_of(s1 * 32, 32), :] + z1_in[k, 0]
        z1_sum[k, 1] = core_sum[k, rows_of(64 + t1 * 32, 32), :] + z1_in[k, 1]
        for cp in z2_copies(k):
            cp.start()

    def stage_z2(k):
        for cp in z2_copies(k):
            cp.wait_recv()
        for h, (keep, base) in enumerate(((s2, row_1), (t2, row_2))):
            total = z1_sum[k, h, rows_of(keep * 16, 16), :] + z2_in[k, h]
            mode_x = (lax.broadcasted_iota(jnp.int32, (16, KC), 1) + k * KC).astype(F32)
            mode_v = (lax.broadcasted_iota(jnp.int32, (16, KC), 0) + base).astype(F32)
            bend_x = mode_x * fac_x * (1.0 / MX)
            bend_v = mode_v * fac_v * (1.0 / MV)
            weight = 1.0 / ((1.0 + bend_x * bend_x) * (1.0 + bend_v * bend_v))
            scale_x = jnp.where(mode_x == 0.0, 1.0 / NX, 2.0 / NX).astype(F32)
            scale_v = jnp.where(mode_v == 0.0, 1.0 / NV, 2.0 / NV).astype(F32)
            block[k, h * 16 : (h + 1) * 16, :] = total * (weight * (scale_x * scale_v))
        for o in range(1, 16):
            plane_copy(k, o).start()

    def stage_plane(k):
        mine = block[k, rows_of((p // 4) * 8, 8), pl.ds(pl.multiple_of((p % 4) * KQ, KQ), KQ)]
        plane_in[k, 0] = mine
        for o in range(1, 16):
            plane_copy(k, o).wait_recv()
        if k == 0:
            for o in range(1, 8):
                copy(
                    coef_own, coef_all.at[(c + 8 - o) % 8], coef_send.at[o], coef_recv.at[o], {"comp": c, "dom": d}
                ).wait_recv()
        own = []
        for g in range(8):
            a = plane_in[k, (p + 16 - 2 * g) % 16]
            b = plane_in[k, (p + 16 - 2 * g - 1) % 16]
            own.append(a + b)
        total = jnp.zeros((8, KQ), F32)
        for g in range(8):
            total = total + coef_all[g][:, 0:1] * own[g]
        for g in range(8):
            back_out[k, g] = total - own[g]
        upd[own_tile(k)] = back_out[k, c]
        for o in range(1, 16):
            back_copy(k, o).start()

    def stage_back(k):
        for o in range(1, 16):
            back_wait(k, o)
        for cp in g2_copies(k):
            cp.start()

    def stage_g2(k):
        g2_waits(k)
        for cp in g1_copies(k):
            cp.start()

    def stage_g1(k):
        g1_waits(k)
        gc_copy(k).start()

    def stage_gc(k):
        gc_wait(k)
        u_hi, u_lo = split(upd[:, cols_of(k)])
        term = dot3(bx_h[:, cols_of(k)], bx_l[:, cols_of(k)], u_hi, u_lo, NT)
        if k == 0:
            corr[...] = term
        else:
            corr[...] += term

    stages = (stage_project, stage_core, stage_z1, stage_z2, stage_plane, stage_back, stage_g2, stage_g1, stage_gc)
    for tick in range(NCH + len(stages) - 1):
        for s in reversed(range(len(stages))):
            if 0 <= tick - s < NCH:
                stages[s](tick - s)

    c_hi, c_lo = split(corr[...])
    for kt in range(TILES // 2):
        cols = slice(kt * 256, (kt + 1) * 256)
        add = dot3(c_hi, c_lo, bv_h[:, cols], bv_l[:, cols], NN)
        for t in range(2):
            part_t = add[:, t * LANES : (t + 1) * LANES]
            fa[2 * kt + t, LEAD : LEAD + ROWS + 8, :] += part_t[0 : ROWS + 8]
            fa[2 * kt + t, LEAD - 8 : LEAD, :] += part_t[ROWS + 8 :]

    rate = set_rates(jnp.float32(1.0))
    step(fa, fb, LEAD - 8, WIDE, rate)

    def store(t, quarter):
        return pltpu.make_async_copy(
            fa.at[t, pl.ds(LEAD + quarter * 96, 96), :],
            out_ref.at[0, pl.ds(quarter * 96, 96), pl.ds(t * LANES, LANES)],
            out_sem.at[quarter, t],
        )

    for quarter in range(4):
        step(fb, fa, LEAD + quarter * 96, 96, rate)
        for t in range(TILES):
            store(t, quarter).start()

    for o in range(1, 8):
        coef_copy(o).wait_send()
    for k in range(NCH):
        core_copy(k).wait_send()
        gc_copy(k).wait_send()
        for group in (z1_copies(k), z2_copies(k), g2_copies(k), g1_copies(k)):
            for cp in group:
                cp.wait_send()
        for o in range(1, 16):
            plane_copy(k, o).wait_send()
            back_copy(k, o).wait_send()
    for quarter in range(4):
        for t in range(TILES):
            store(t, quarter).wait()


def body(densities, levels, coeffs):
    dma = pltpu.SemaphoreType.DMA
    vmem = pltpu.VMEM
    return pl.pallas_call(
        kernel,
        out_shape=jax.ShapeDtypeStruct((1, ROWS, NV), F32),
        in_specs=[
            pl.BlockSpec(memory_space=pltpu.SMEM),
            pl.BlockSpec(memory_space=pltpu.SMEM),
            pl.BlockSpec(memory_space=pl.ANY),
        ],
        out_specs=pl.BlockSpec(memory_space=pl.ANY),
        scratch_shapes=[
            vmem((TILES, PLANE_ROWS, LANES), F32),
            vmem((TILES, PLANE_ROWS, LANES), F32),
            vmem((TILES, 8, LANES), F32),
            vmem((TILES, 8, LANES), F32),
            vmem((WIDE, MX), BF16),
            vmem((WIDE, MX), BF16),
            vmem((MV, NV), BF16),
            vmem((MV, NV), BF16),
            vmem((MV, ROWS), BF16),
            vmem((MV, ROWS), BF16),
            vmem((MV, MX), F32),
            vmem((NCH, 128, KC), F32),
            vmem((NCH, 128, KC), F32),
            vmem((NCH, 2, 32, KC), F32),
            vmem((NCH, 2, 32, KC), F32),
            vmem((NCH, 2, 16, KC), F32),
            vmem((NCH, 32, KC), F32),
            vmem((NCH, 16, 8, KQ), F32),
            vmem((NCH, 8, 8, KQ), F32),
            vmem((MV, MX), F32),
            vmem((WIDE, MV), F32),
            vmem((8, LANES), F32),
            vmem((8, 8, LANES), F32),
            dma((TILES,)),
            dma((4, TILES)),
            dma((2,)),
            dma((2,)),
            dma((8,)),
            dma((8,)),
            dma((NCH,)),
            dma((NCH,)),
            dma((NCH, 2)),
            dma((NCH, 2)),
            dma((NCH, 2)),
            dma((NCH, 2)),
            dma((NCH, 16)),
            dma((NCH, 16)),
            dma((NCH, 16)),
            dma((NCH, 16)),
            dma((NCH, 2)),
            dma((NCH, 2)),
            dma((NCH, 2)),
            dma((NCH, 2)),
            dma((NCH,)),
            dma((NCH,)),
        ],
        compiler_params=pltpu.CompilerParams(
            collective_id=0, has_side_effects=True, vmem_limit_bytes=60 * 1024 * 1024
        ),
        name="window",
    )(levels, coeffs, densities)


def solution(mesh):
    placed = (P("comp", "dom", None), P("comp", None), P("comp"))
    return jax.shard_map(
        body, mesh=mesh, in_specs=placed, out_specs=P("comp", "dom", None), check_vma=False
    )
```

profile of v0, /device:TPU:1, one launch (start us, length us, event | category | flops | bytes accessed | tf_op | source)
XLA Modules:
  0.0 108.7 jit_solution(2197533132883776473)
XLA Ops:
  0.7 104.1 %window.1 = f32[1,384,2048]{2,1,0:T(8,128)} custom-call(s32[1,2]{1,0:T(1,128)} %lev_ref.1, s32[1]{0:T(128)S(6)} %copy.5.coef_ref, f32[1,384,2048]{2,1,0:T(8,128)} %dens_ref.1), custom_call_target="tpu_custom_call" | custom-call | tf_op jit(solution)/shard_map/window/pallas_call | solution.py:569
  104.8 3.9 %copy.6 = f32[1,384,2048]{2,1,0:T(8,128)} copy(f32[1,384,2048]{2,1,0:T(8,128)} %window.1) | data formatting | bytes 6291456
where the time goes:
time: 109 us
  Pallas kernels  104 us (95%)
  local copies, waits for them, and re-layouts  3.91 us (4%)
    pallas_call x1, Pallas kernels, body(): pl.pallas_call(kernel, out_shape=jax.ShapeDtypeStruct((1, ROWS, NV), F32)...  104 us
    unnamed x1, local copies, waits for them, and re-layouts  3.91 us

commit v1 on v0

--- a/solution.py
+++ b/solution.py
@@ -18,10 +18,12 @@
 LANES = 128
 TILES = NV // LANES
 HALO = 16
-LEAD = 24
-PLANE_ROWS = 432
-WIDE = 400
-NCH = 4
+SPAN = 4
+LEAD = 64
+WIDE = SPAN * LANES
+PAD = 8
+BLOCKS = 8
+NCH = 2
 KC = MX // NCH
 KQ = KC // 4
 MESH = pl.DeviceIdType.MESH
@@ -63,6 +65,9 @@
     return hi, (x - hi.astype(F32)).astype(BF16)
 
 
+scope = jax.named_scope
+
+
 def dot3(a_hi, a_lo, b_hi, b_lo, dims):
     def dot(a, b):
         return lax.dot_general(a, b, (dims, ((), ())), preferred_element_type=F32)
@@ -79,14 +84,15 @@
     coef_ref,
     dens_ref,
     out_ref,
+    cells,
     fa,
     fb,
-    al_ref,
-    be_ref,
     bx_h,
     bx_l,
     bv_h,
     bv_l,
+    bt_h,
+    bt_l,
     red_h,
     red_l,
     part,
@@ -157,7 +163,7 @@
     def load(t):
         return pltpu.make_async_copy(
             dens_ref.at[0, :, pl.ds(t * LANES, LANES)],
-            fa.at[t, pl.ds(LEAD, ROWS), :],
+            cells.at[t, pl.ds(LEAD, ROWS), :],
             in_sem.at[t],
         )
 
@@ -177,7 +183,7 @@
     lane = lax.broadcasted_iota(jnp.int32, (16, LANES), 1)
     row16 = lax.broadcasted_iota(jnp.int32, (16, LANES), 0)
 
-    def velocity_basis(i, _):
+    def mode_rows(i, _):
         mode = (row16 + i * 16).astype(F32)
         r0 = pl.multiple_of(i * 16, 16)
         for t in range(TILES):
@@ -188,23 +194,60 @@
             bv_l[pl.ds(r0, 16), t * LANES : (t + 1) * LANES] = lo
         return 0
 
-    lax.fori_loop(0, MV // 16, velocity_basis, 0)
-
-    for t in range(TILES):
-        load(t).wait()
-    pl.semaphore_wait(barrier, 20)
+    def cell_rows(i, _):
+        for b in range(4):
+            r0 = pl.multiple_of(i * 64 + b * 16, 16)
+            angle = np.float32(np.pi) * ((row16 + r0).astype(F32) + 0.5)
+            for t in range(MV // LANES):
+                mode = (lane + t * LANES).astype(F32)
+                phase = (angle * mode) * np.float32(1.0 / NV)
+                hi, lo = split(cosine(phase))
+                bt_h[pl.ds(r0, 16), t * LANES : (t + 1) * LANES] = hi
+                bt_l[pl.ds(r0, 16), t * LANES : (t + 1) * LANES] = lo
+        return 0
+
+    def space_basis(k, i):
+        local = (row16 + (i % 8) * 16) * SPAN + i // 8 - LEAD
+        cell = local + d * ROWS
+        cell = jnp.where(cell < 0, cell + NX, cell)
+        cell = jnp.where(cell >= NX, cell - NX, cell)
+        angle = np.float32(np.pi) * (cell.astype(F32) + 0.5)
+        r0 = pl.multiple_of(i * 16, 16)
+        for t in range(k * KC // LANES, (k + 1) * KC // LANES):
+            mode = (lane + t * LANES).astype(F32)
+            phase = (angle * mode) * np.float32(1.0 / NX)
+            hi, lo = split(cosine(phase))
+            bx_h[pl.ds(r0, 16), t * LANES : (t + 1) * LANES] = hi
+            bx_l[pl.ds(r0, 16), t * LANES : (t + 1) * LANES] = lo
+
+    def fill_space_basis(k):
+        def run(i, _):
+            space_basis(k, 2 * i)
+            space_basis(k, 2 * i + 1)
+            return 0
+
+        lax.fori_loop(0, WIDE // 32, run, 0)
+
+    with scope("A_bv"):
+        lax.fori_loop(0, MV // 16, mode_rows, 0)
+        fill_space_basis(0)
+
+    with scope('B_barrier'):
+        for t in range(TILES):
+            load(t).wait()
+        pl.semaphore_wait(barrier, 20)
 
     halo_up = pltpu.make_async_remote_copy(
-        src_ref=fa.at[:, pl.ds(LEAD, HALO), :],
-        dst_ref=fa.at[:, pl.ds(LEAD + ROWS, HALO), :],
+        src_ref=cells.at[pl.ds(0, 9), pl.ds(LEAD, HALO), :],
+        dst_ref=cells.at[pl.ds(0, 9), pl.ds(LEAD + ROWS, HALO), :],
         send_sem=halo_send.at[0],
         recv_sem=halo_recv.at[0],
         device_id=dom_id(prv),
         device_id_type=MESH,
     )
     halo_down = pltpu.make_async_remote_copy(
-        src_ref=fa.at[:, pl.ds(LEAD + ROWS - HALO, HALO), :],
-        dst_ref=fa.at[:, pl.ds(LEAD - HALO, HALO), :],
+        src_ref=cells.at[pl.ds(7, 9), pl.ds(LEAD + ROWS - HALO, HALO), :],
+        dst_ref=cells.at[pl.ds(7, 9), pl.ds(LEAD - HALO, HALO), :],
         send_sem=halo_send.at[1],
         recv_sem=halo_recv.at[1],
         device_id=dom_id(nxt),
@@ -226,79 +269,102 @@
     for o in range(1, 8):
         coef_copy(o).start()
 
-    def space_basis(i, _):
-        local = row16 + i * 16
-        local = jnp.where(local >= ROWS + 8, local - WIDE, local)
-        cell = local + d * ROWS
-        cell = jnp.where(cell < 0, cell + NX, cell)
-        cell = jnp.where(cell >= NX, cell - NX, cell)
-        angle = np.float32(np.pi) * (cell.astype(F32) + 0.5)
-        r0 = pl.multiple_of(i * 16, 16)
-        for t in range(TILES):
-            mode = (lane + t * LANES).astype(F32)
-            phase = (angle * mode) * np.float32(1.0 / NX)
-            hi, lo = split(cosine(phase))
-            bx_h[pl.ds(r0, 16), t * LANES : (t + 1) * LANES] = hi
-            bx_l[pl.ds(r0, 16), t * LANES : (t + 1) * LANES] = lo
-        return 0
-
-    lax.fori_loop(0, WIDE // 16, space_basis, 0)
-
-    lane8 = lax.broadcasted_iota(jnp.int32, (8, LANES), 1)
-
-    def set_rates(active):
-        for t in range(TILES):
-            cell = (lane8 + t * LANES).astype(F32)
-            speed = jnp.abs(-1.0 + (2.0 * cell + 1.0) / NV) * courant
-            al_ref[t] = 1.0 - active * (2.0 * diffusion + speed)
-            be_ref[t] = active * speed
-        return active * diffusion
-
-    first_lane = lane == 0
-    last_lane = lane == LANES - 1
-
-    def step(src, dst, start, count, rate):
-        def rows(i, _):
-            r = start + i * 16
-            r8 = pl.multiple_of(r, 8)
-            f = [src[t, pl.ds(r8, 16), :] for t in range(TILES)]
-            rl = [pltpu.roll(x, 1, 1) for x in f]
-            rr = [pltpu.roll(x, LANES - 1, 1) for x in f]
-            for t in range(TILES):
-                left = jnp.where(first_lane, rl[t - 1] if t > 0 else f[0], rl[t])
-                right = jnp.where(last_lane, rr[t + 1] if t < TILES - 1 else f[t], rr[t])
-                shifted = src[t, pl.ds(r + 1 if t < TILES // 2 else r - 1, 16), :]
-                al = jnp.concatenate([al_ref[t]] * 2, axis=0)
-                be = jnp.concatenate([be_ref[t]] * 2, axis=0)
-                dst[t, pl.ds(r8, 16), :] = al * f[t] + be * shifted + rate * (left + right)
+    with scope("C_bx"):
+        for k in range(1, NCH):
+            fill_space_basis(k)
+
+    def edges(dst):
+        for q in range(SPAN):
+            dst[q, PAD - 1 : PAD, :] = dst[q, PAD : PAD + 1, :]
+            dst[q, PAD + NV : PAD + NV + 1, :] = dst[q, PAD + NV - 1 : PAD + NV, :]
+
+    row_v = lax.broadcasted_iota(jnp.int32, (16, LANES), 0)
+    offsets = (2.0 * row_v.astype(F32) + 1.0) / NV - 1.0
+
+    def step(src, dst, active, scale, unit):
+        rate = active * diffusion
+        share = (1.0 / diffusion) if unit else scale
+        keep = (1.0 - 2.0 * rate) * share
+        pace = active * courant * share
+        side = rate * share
+        size = 16 * BLOCKS
+
+        def rows(upper):
+            base = NV // 2 if upper else 0
+            edge = SPAN - 1 if upper else 0
+            count = NV // 2 // size
+
+            def turned(i):
+                r0 = pl.multiple_of(i * size + base + PAD, 8)
+                return tuple(
+                    pltpu.roll(src[edge, pl.ds(r0 + b * 16, 16), :], 1 if upper else LANES - 1, 1)
+                    for b in range(BLOCKS)
+                )
+
+            def run(i, ends):
+                ahead = turned((i + 1) % count)
+                for b in range(BLOCKS):
+                    first = i * size + (base + b * 16)
+                    r = pl.multiple_of(first + PAD, 8)
+                    velocity = offsets + first.astype(F32) * (2.0 / NV)
+                    be = velocity * (pace if upper else -pace)
+                    al = keep - be
+                    f = [src[q, pl.ds(r, 16), :] for q in range(SPAN)]
+                    shifted = [ends[b]] + f[:-1] if upper else f[1:] + [ends[b]]
+                    for q in range(SPAN):
+                        pair = src[q, pl.ds(r - 1, 16), :] + src[q, pl.ds(r + 1, 16), :]
+                        if not unit:
+                            pair = side * pair
+                        dst[q, pl.ds(r, 16), :] = al * f[q] + be * shifted[q] + pair
+                return ahead
+
+            lax.fori_loop(0, count, run, turned(0))
+
+        rows(False)
+        rows(True)
+        edges(dst)
+
+    with scope('D_halo'):
+        halo_up.wait_recv()
+        halo_down.wait_recv()
+        halo_up.wait_send()
+        halo_down.wait_send()
+    with scope("E_turn"):
+
+        def turn_in(t, _):
+            for q in range(SPAN):
+                tile = cells[t, pl.ds(q, LANES, stride=SPAN), :]
+                fa[q, pl.ds(pl.multiple_of(PAD + t * LANES, 8), LANES), :] = tile.T
             return 0
 
-        lax.fori_loop(0, count // 16, rows, 0)
-
-    rate = set_rates(jnp.float32(1.0))
-    halo_up.wait_recv()
-    halo_down.wait_recv()
-    halo_up.wait_send()
-    halo_down.wait_send()
+        lax.fori_loop(0, TILES, turn_in, 0, unroll=4)
+        edges(fa)
     src, dst = fa, fb
+    scale = diffusion * diffusion
+    scale = scale * scale * diffusion
     for s in range(PRE):
-        if s >= PRE - 3:
-            rate = set_rates(jnp.where(lev_x > s - (PRE - 3), 1.0, 0.0).astype(F32))
-        if s == 0:
-            step(src, dst, LEAD - HALO, ROWS + 2 * HALO, rate)
-        else:
-            step(src, dst, LEAD - 8, WIDE, rate)
+        with scope("E_step"):
+            if s < PRE - 3:
+                step(src, dst, 1.0, 1.0, True)
+            else:
+                active = jnp.where(lev_x > s - (PRE - 3), 1.0, 0.0).astype(F32)
+                step(src, dst, active, scale if s == PRE - 3 else 1.0, False)
         src, dst = dst, src
 
-    reduced = jnp.zeros((ROWS, MV), F32)
-    for kt in range(TILES // 2):
-        block_f = jnp.concatenate([fa[2 * kt, LEAD : LEAD + ROWS, :], fa[2 * kt + 1, LEAD : LEAD + ROWS, :]], axis=1)
-        a_hi, a_lo = split(block_f)
-        cols = slice(kt * 256, (kt + 1) * 256)
-        reduced = reduced + dot3(a_hi, a_lo, bv_h[:, cols], bv_l[:, cols], NT)
-    hi, lo = split(reduced.T)
-    red_h[...] = hi
-    red_l[...] = lo
+    with scope("F_reduced"):
+        own_lanes = lax.broadcasted_iota(jnp.int32, (MV, 2 * LANES), 1) % LANES
+        own_lanes = (own_lanes >= LEAD // SPAN) & (own_lanes < (LEAD + ROWS) // SPAN)
+        for half in range(2):
+            reduced = jnp.zeros((MV, 2 * LANES), F32)
+            for kt in range(TILES // 2):
+                cut = slice(PAD + kt * 256, PAD + (kt + 1) * 256)
+                cols = slice(kt * 256, (kt + 1) * 256)
+                f = jnp.concatenate([fa[2 * half, cut, :], fa[2 * half + 1, cut, :]], axis=1)
+                f_hi, f_lo = split(f)
+                reduced = reduced + dot3(bv_h[:, cols], bv_l[:, cols], f_hi, f_lo, NN)
+            hi, lo = split(jnp.where(own_lanes, reduced, 0.0))
+            red_h[:, half * 256 : (half + 1) * 256] = hi
+            red_l[:, half * 256 : (half + 1) * 256] = lo
 
     def rows_of(base, size):
         return pl.ds(pl.multiple_of(base, size), size)
@@ -370,8 +436,6 @@
         )
 
     my_tile = p // 4
-    my_row = jnp.where(my_tile < 2, row_1 + my_tile * 8, row_2 + (my_tile - 2) * 8)
-    del my_row
     half = my_tile // 2
     own_row = row_1 + half * (row_2 - row_1) + (my_tile % 2) * 8
     own_lane = (p % 4) * KQ
@@ -436,7 +500,7 @@
     fac_v = power(lev_v)
 
     def stage_project(k):
-        part[:, cols_of(k)] = dot3(red_h[...], red_l[...], bx_h[0:ROWS, cols_of(k)], bx_l[0:ROWS, cols_of(k)], NN)
+        part[:, cols_of(k)] = dot3(red_h[...], red_l[...], bx_h[:, cols_of(k)], bx_l[:, cols_of(k)], NN)
         core_copy(k).start()
 
     def stage_core(k):
@@ -511,7 +575,7 @@
     def stage_gc(k):
         gc_wait(k)
         u_hi, u_lo = split(upd[:, cols_of(k)])
-        term = dot3(bx_h[:, cols_of(k)], bx_l[:, cols_of(k)], u_hi, u_lo, NT)
+        term = dot3(u_hi, u_lo, bx_h[:, cols_of(k)], bx_l[:, cols_of(k)], NT)
         if k == 0:
             corr[...] = term
         else:
@@ -521,46 +585,60 @@
     for tick in range(NCH + len(stages) - 1):
         for s in reversed(range(len(stages))):
             if 0 <= tick - s < NCH:
-                stages[s](tick - s)
-
-    c_hi, c_lo = split(corr[...])
-    for kt in range(TILES // 2):
-        cols = slice(kt * 256, (kt + 1) * 256)
-        add = dot3(c_hi, c_lo, bv_h[:, cols], bv_l[:, cols], NN)
-        for t in range(2):
-            part_t = add[:, t * LANES : (t + 1) * LANES]
-            fa[2 * kt + t, LEAD : LEAD + ROWS + 8, :] += part_t[0 : ROWS + 8]
-            fa[2 * kt + t, LEAD - 8 : LEAD, :] += part_t[ROWS + 8 :]
-
-    rate = set_rates(jnp.float32(1.0))
-    step(fa, fb, LEAD - 8, WIDE, rate)
-
-    def store(t, quarter):
+                with scope('G_%d_%s' % (tick - s, stages[s].__name__)):
+                    stages[s](tick - s)
+        if tick == 1:
+            with scope("G_bt"):
+                lax.fori_loop(0, NV // 64, cell_rows, 0)
+
+    with scope("H_expand"):
+        for half in range(2):
+            c_hi, c_lo = split(corr[:, half * 256 : (half + 1) * 256])
+            for kt in range(TILES // 2):
+                rows = slice(kt * 256, (kt + 1) * 256)
+                cut = slice(PAD + kt * 256, PAD + (kt + 1) * 256)
+                add = dot3(bt_h[rows, :], bt_l[rows, :], c_hi, c_lo, NN)
+                fa[2 * half, cut, :] += add[:, :LANES]
+                fa[2 * half + 1, cut, :] += add[:, LANES:]
+        edges(fa)
+
+    with scope("I_post"):
+        step(fa, fb, 1.0, 1.0, True)
+        step(fb, fa, 1.0, diffusion, False)
+
+    def store(t):
         return pltpu.make_async_copy(
-            fa.at[t, pl.ds(LEAD + quarter * 96, 96), :],
-            out_ref.at[0, pl.ds(quarter * 96, 96), pl.ds(t * LANES, LANES)],
-            out_sem.at[quarter, t],
-        )
-
-    for quarter in range(4):
-        step(fb, fa, LEAD + quarter * 96, 96, rate)
+            cells.at[t, pl.ds(LEAD, ROWS), :],
+            out_ref.at[0, :, pl.ds(pl.multiple_of(t * LANES, LANES), LANES)],
+            out_sem.at[t],
+        )
+
+    with scope("J_turn"):
+        low, high = LEAD // SPAN, (LEAD + ROWS) // SPAN
+
+        def turn_out(t, _):
+            for q in range(SPAN):
+                tile = fa[q, pl.ds(pl.multiple_of(PAD + t * LANES, 8), LANES), :].T
+                cells[t, pl.ds(LEAD + q, high - low, stride=SPAN), :] = tile[low:high]
+            store(t).start()
+            return 0
+
+        lax.fori_loop(0, TILES, turn_out, 0, unroll=4)
+
+    with scope('K_tail'):
+        for o in range(1, 8):
+            coef_copy(o).wait_send()
+        for k in range(NCH):
+            core_copy(k).wait_send()
+            gc_copy(k).wait_send()
+            for group in (z1_copies(k), z2_copies(k), g2_copies(k), g1_copies(k)):
+                for cp in group:
+                    cp.wait_send()
+            for o in range(1, 16):
+                plane_copy(k, o).wait_send()
+                back_copy(k, o).wait_send()
         for t in range(TILES):
-            store(t, quarter).start()
-
-    for o in range(1, 8):
-        coef_copy(o).wait_send()
-    for k in range(NCH):
-        core_copy(k).wait_send()
-        gc_copy(k).wait_send()
-        for group in (z1_copies(k), z2_copies(k), g2_copies(k), g1_copies(k)):
-            for cp in group:
-                cp.wait_send()
-        for o in range(1, 16):
-            plane_copy(k, o).wait_send()
-            back_copy(k, o).wait_send()
-    for quarter in range(4):
-        for t in range(TILES):
-            store(t, quarter).wait()
+            store(t).wait()
 
 
 def body(densities, levels, coeffs):
@@ -576,16 +654,17 @@
         ],
         out_specs=pl.BlockSpec(memory_space=pl.ANY),
         scratch_shapes=[
-            vmem((TILES, PLANE_ROWS, LANES), F32),
-            vmem((TILES, PLANE_ROWS, LANES), F32),
-            vmem((TILES, 8, LANES), F32),
-            vmem((TILES, 8, LANES), F32),
+            vmem((TILES, WIDE, LANES), F32),
+            vmem((SPAN, NV + 2 * PAD, LANES), F32),
+            vmem((SPAN, NV + 2 * PAD, LANES), F32),
             vmem((WIDE, MX), BF16),
             vmem((WIDE, MX), BF16),
             vmem((MV, NV), BF16),
             vmem((MV, NV), BF16),
-            vmem((MV, ROWS), BF16),
-            vmem((MV, ROWS), BF16),
+            vmem((NV, MV), BF16),
+            vmem((NV, MV), BF16),
+            vmem((MV, WIDE), BF16),
+            vmem((MV, WIDE), BF16),
             vmem((MV, MX), F32),
             vmem((NCH, 128, KC), F32),
             vmem((NCH, 128, KC), F32),
@@ -596,11 +675,11 @@
             vmem((NCH, 16, 8, KQ), F32),
             vmem((NCH, 8, 8, KQ), F32),
             vmem((MV, MX), F32),
-            vmem((WIDE, MV), F32),
+            vmem((MV, WIDE), F32),
             vmem((8, LANES), F32),
             vmem((8, 8, LANES), F32),
             dma((TILES,)),
-            dma((4, TILES)),
+            dma((TILES,)),
             dma((2,)),
             dma((2,)),
             dma((8,)),

time: 109 us -> 88.9 us (0.82)
  Pallas kernels: 104 us -> 84.2 us
    pallas_call x1, Pallas kernels: 104 us -> 84.2 us  [body(): pl.pallas_call(kernel, out_shape=jax.ShapeDtypeStruct((1, ROWS, NV), F32)...]
where the time goes in v1:
time: 88.9 us; the launch traced here: 88.7 us
  Pallas kernels  84.2 us (95%)
  local copies, waits for them, and re-layouts  3.91 us (4%)
    pallas_call x1, Pallas kernels, body(): pl.pallas_call(kernel, out_shape=jax.ShapeDtypeStruct((1, ROWS, NV), F32)...  84.2 us
    unnamed x1, local copies, waits for them, and re-layouts  3.91 us

profile of v1, /device:TPU:1, one launch (start us, length us, event | category | flops | bytes accessed | tf_op | source)
XLA Modules:
  0.0 88.7 jit_solution(3503863414705330479)
XLA Ops:
  0.7 84.2 %window.1 = f32[1,384,2048]{2,1,0:T(8,128)} custom-call(s32[1,2]{1,0:T(1,128)} %lev_ref.1, s32[1]{0:T(128)S(6)} %copy.5.coef_ref, f32[1,384,2048]{2,1,0:T(8,128)} %dens_ref.1), custom_call_target="tpu_custom_call" | custom-call | tf_op jit(solution)/shard_map/window/pallas_call | solution.py:647
  84.8 3.9 %copy.6 = f32[1,384,2048]{2,1,0:T(8,128)} copy(f32[1,384,2048]{2,1,0:T(8,128)} %window.1) | data formatting | bytes 6291456

commit v2 on v1

v2 whole, which is shorter than its diff:
```python
import functools

import jax
import jax.numpy as jnp
import numpy as np
from jax import lax
from jax.experimental import pallas as pl
from jax.experimental.pallas import tpu as pltpu
from jax.sharding import PartitionSpec as P

MX = 2048
MV = 256
PRE = 8
POST = 2
NV = 2048
ROWS = 384
NX = 6144
LANES = 128
TILES = NV // LANES
HALO = 16
SPAN = 4
LEAD = 64
WIDE = SPAN * LANES
PAD = 8
NCH = 2
KC = MX // NCH
KQ = KC // 4
MESH = pl.DeviceIdType.MESH
F32 = jnp.float32
BF16 = jnp.bfloat16

TWO_PI_HI = float(np.float32(6.28125))
TWO_PI_LO = float(np.float32(2.0 * np.pi - 6.28125))
INV_TWO_PI = float(np.float32(1.0 / (2.0 * np.pi)))


def sine_terms():
    count = 6
    nodes = np.cos(np.pi * (np.arange(64) + 0.5) / 128)
    r = np.pi * nodes
    u = r * r
    basis = np.stack([u**i for i in range(count)], axis=1)
    target = np.sqrt(2.0) * np.sin(r / 2) / r
    terms, *_ = np.linalg.lstsq(basis * r[:, None], target * r, rcond=None)
    return [float(np.float32(t)) for t in terms]


SINE_TERMS = sine_terms()


def cosine(phase):
    turns = jnp.round(phase * INV_TWO_PI)
    r = (phase - turns * TWO_PI_HI) - turns * TWO_PI_LO
    u = r * r
    s = jnp.full_like(u, SINE_TERMS[-1])
    for term in SINE_TERMS[-2::-1]:
        s = s * u + term
    s = s * r
    return 1.0 - s * s


def split(x):
    hi = x.astype(BF16)
    return hi, (x - hi.astype(F32)).astype(BF16)


scope = jax.named_scope


def dot3(a_hi, a_lo, b_hi, b_lo, dims):
    def dot(a, b):
        return lax.dot_general(a, b, (dims, ((), ())), preferred_element_type=F32)

    return dot(a_hi, b_hi) + dot(a_hi, b_lo) + dot(a_lo, b_hi)


NN = ((1,), (0,))
NT = ((1,), (1,))


def kernel(
    lev_ref,
    coef_ref,
    dens_ref,
    out_ref,
    cells,
    fa,
    fb,
    bx_h,
    bx_l,
    bv_h,
    bv_l,
    bt_h,
    bt_l,
    red_h,
    red_l,
    part,
    core_in,
    core_sum,
    z1_in,
    z1_sum,
    z2_in,
    block,
    plane_in,
    back_out,
    upd,
    corr,
    coef_own,
    coef_all,
    in_sem,
    out_sem,
    halo_send,
    halo_recv,
    coef_send,
    coef_recv,
    core_send,
    core_recv,
    z1_send,
    z1_recv,
    z2_send,
    z2_recv,
    plane_send,
    plane_recv,
    back_send,
    back_recv,
    g2_send,
    g2_recv,
    g1_send,
    g1_recv,
    gc_send,
    gc_recv,
):
    c = lax.axis_index("comp")
    d = lax.axis_index("dom")
    z = d // 4
    xh = (d // 2) % 2
    core = d % 2
    p = c * 2 + xh
    nxt = (d + 1) % 16
    prv = (d + 15) % 16
    peer = d + 1 - 2 * core
    za = (z + 1 - 2 * (z % 2)) * 4 + d % 4
    zb = (3 - z) * 4 + d % 4
    s1 = (z % 2 + z // 2) % 2
    s2 = z // 2
    t1 = z // 2
    t2 = s1

    def dom_id(dom):
        return {"comp": c, "dom": dom}

    def plane_id(q):
        return {"comp": q // 2, "dom": z * 4 + (q % 2) * 2 + core}

    barrier = pltpu.get_barrier_semaphore()
    for dom in (nxt, prv, peer, za, zb):
        pl.semaphore_signal(barrier, inc=1, device_id=dom_id(dom), device_id_type=MESH)
    for o in range(1, 16):
        q = (p + o) % 16
        pl.semaphore_signal(barrier, inc=1, device_id=plane_id(q), device_id_type=MESH)

    def load(t):
        return pltpu.make_async_copy(
            dens_ref.at[0, :, pl.ds(t * LANES, LANES)],
            cells.at[t, pl.ds(LEAD, ROWS), :],
            in_sem.at[t],
        )

    for t in range(TILES):
        load(t).start()

    lev_x = lev_ref[0, 0]
    lev_v = lev_ref[0, 1]
    courant = 0.3 + lev_x.astype(F32) / 15.0
    diffusion = 0.1 + lev_v.astype(F32) / 30.0
    coef_own[...] = jnp.full((8, LANES), coef_ref[0].astype(F32), F32)
    coef_all[c] = coef_own[...]

    def power(level):
        return jnp.where(level == 0, 8.0, jnp.where(level == 1, 4.0, jnp.where(level == 2, 2.0, 1.0))).astype(F32)

    lane = lax.broadcasted_iota(jnp.int32, (16, LANES), 1)
    row16 = lax.broadcasted_iota(jnp.int32, (16, LANES), 0)

    def mode_rows(i, _):
        mode = (row16 + i * 16).astype(F32)
        r0 = pl.multiple_of(i * 16, 16)
        for t in range(TILES):
            cell = (lane + t * LANES).astype(F32)
            phase = ((np.float32(np.pi) * (cell + 0.5)) * mode) * np.float32(1.0 / NV)
            hi, lo = split(cosine(phase))
            bv_h[pl.ds(r0, 16), t * LANES : (t + 1) * LANES] = hi
            bv_l[pl.ds(r0, 16), t * LANES : (t + 1) * LANES] = lo
        return 0

    def cell_rows(i, _):
        for b in range(4):
            r0 = pl.multiple_of(i * 64 + b * 16, 16)
            angle = np.float32(np.pi) * ((row16 + r0).astype(F32) + 0.5)
            for t in range(MV // LANES):
                mode = (lane + t * LANES).astype(F32)
                phase = (angle * mode) * np.float32(1.0 / NV)
                hi, lo = split(cosine(phase))
                bt_h[pl.ds(r0, 16), t * LANES : (t + 1) * LANES] = hi
                bt_l[pl.ds(r0, 16), t * LANES : (t + 1) * LANES] = lo
        return 0

    def space_basis(k, i):
        local = (row16 + (i % 8) * 16) * SPAN + i // 8 - LEAD
        cell = local + d * ROWS
        cell = jnp.where(cell < 0, cell + NX, cell)
        cell = jnp.where(cell >= NX, cell - NX, cell)
        angle = np.float32(np.pi) * (cell.astype(F32) + 0.5)
        r0 = pl.multiple_of(i * 16, 16)
        for t in range(k * KC // LANES, (k + 1) * KC // LANES):
            mode = (lane + t * LANES).astype(F32)
            phase = (angle * mode) * np.float32(1.0 / NX)
            hi, lo = split(cosine(phase))
            bx_h[pl.ds(r0, 16), t * LANES : (t + 1) * LANES] = hi
            bx_l[pl.ds(r0, 16), t * LANES : (t + 1) * LANES] = lo

    def fill_space_basis(k):
        def run(i, _):
            space_basis(k, 2 * i)
            space_basis(k, 2 * i + 1)
            return 0

        lax.fori_loop(0, WIDE // 32, run, 0)

    with scope("A_bv"):
        lax.fori_loop(0, MV // 16, mode_rows, 0)
        fill_space_basis(0)

    with scope('B_barrier'):
        for t in range(TILES):
            load(t).wait()
        pl.semaphore_wait(barrier, 20)

    halo_up = pltpu.make_async_remote_copy(
        src_ref=cells.at[pl.ds(0, 9), pl.ds(LEAD, HALO), :],
        dst_ref=cells.at[pl.ds(0, 9), pl.ds(LEAD + ROWS, HALO), :],
        send_sem=halo_send.at[0],
        recv_sem=halo_recv.at[0],
        device_id=dom_id(prv),
        device_id_type=MESH,
    )
    halo_down = pltpu.make_async_remote_copy(
        src_ref=cells.at[pl.ds(7, 9), pl.ds(LEAD + ROWS - HALO, HALO), :],
        dst_ref=cells.at[pl.ds(7, 9), pl.ds(LEAD - HALO, HALO), :],
        send_sem=halo_send.at[1],
        recv_sem=halo_recv.at[1],
        device_id=dom_id(nxt),
        device_id_type=MESH,
    )
    halo_up.start()
    halo_down.start()

    def coef_copy(o):
        return pltpu.make_async_remote_copy(
            src_ref=coef_own,
            dst_ref=coef_all.at[c],
            send_sem=coef_send.at[o],
            recv_sem=coef_recv.at[o],
            device_id={"comp": (c + o) % 8, "dom": d},
            device_id_type=MESH,
        )

    for o in range(1, 8):
        coef_copy(o).start()

    with scope("C_bx"):
        for k in range(1, NCH):
            fill_space_basis(k)

    def edges(dst):
        for q in range(SPAN):
            dst[q, PAD - 1 : PAD, :] = dst[q, PAD : PAD + 1, :]
            dst[q, PAD + NV : PAD + NV + 1, :] = dst[q, PAD + NV - 1 : PAD + NV, :]

    row_v = lax.broadcasted_iota(jnp.int32, (16, LANES), 0)
    offsets = (2.0 * row_v.astype(F32) + 1.0) / NV - 1.0

    def step(src, dst, active):
        rate = active * diffusion
        keep = 1.0 - 2.0 * rate
        pace = active * courant

        def part_of(first, upper):
            r = first + PAD
            velocity = offsets + first * (2.0 / NV)
            be = velocity * (pace if upper else -pace)
            al = keep - be
            f = [src[q, r : r + 16, :] for q in range(SPAN)]
            if upper:
                shifted = [pltpu.roll(f[SPAN - 1], 1, 1)] + f[:-1]
            else:
                shifted = f[1:] + [pltpu.roll(f[0], LANES - 1, 1)]
            for q in range(SPAN):
                pair = src[q, r - 1 : r + 15, :] + src[q, r + 1 : r + 17, :]
                dst[q, r : r + 16, :] = al * f[q] + be * shifted[q] + rate * pair

        for first in range(0, NV, 16):
            part_of(first, first >= NV // 2)
        edges(dst)

    with scope('D_halo'):
        halo_up.wait_recv()
        halo_down.wait_recv()
        halo_up.wait_send()
        halo_down.wait_send()
    with scope("E_turn"):

        def turn_in(t, _):
            for q in range(SPAN):
                tile = cells[t, pl.ds(q, LANES, stride=SPAN), :]
                fa[q, pl.ds(pl.multiple_of(PAD + t * LANES, 8), LANES), :] = tile.T
            return 0

        lax.fori_loop(0, TILES, turn_in, 0, unroll=4)
        edges(fa)
    def correct():
        with scope("F_reduced"):
            own_lanes = lax.broadcasted_iota(jnp.int32, (MV, 2 * LANES), 1) % LANES
            own_lanes = (own_lanes >= LEAD // SPAN) & (own_lanes < (LEAD + ROWS) // SPAN)
            for half in range(2):
                reduced = jnp.zeros((MV, 2 * LANES), F32)
                for kt in range(TILES // 2):
                    cut = slice(PAD + kt * 256, PAD + (kt + 1) * 256)
                    cols = slice(kt * 256, (kt + 1) * 256)
                    f = jnp.concatenate([fa[2 * half, cut, :], fa[2 * half + 1, cut, :]], axis=1)
                    f_hi, f_lo = split(f)
                    reduced = reduced + dot3(bv_h[:, cols], bv_l[:, cols], f_hi, f_lo, NN)
                hi, lo = split(jnp.where(own_lanes, reduced, 0.0))
                red_h[:, half * 256 : (half + 1) * 256] = hi
                red_l[:, half * 256 : (half + 1) * 256] = lo

        def rows_of(base, size):
            return pl.ds(pl.multiple_of(base, size), size)

        def copy(src_ref, dst_ref, send, recv, dev):
            return pltpu.make_async_remote_copy(
                src_ref=src_ref, dst_ref=dst_ref, send_sem=send, recv_sem=recv, device_id=dev, device_id_type=MESH
            )

        def cols_of(k):
            return slice(k * KC, (k + 1) * KC)

        def core_copy(k):
            return copy(
                part.at[rows_of((1 - core) * 128, 128), pl.ds(k * KC, KC)],
                core_in.at[k],
                core_send.at[k],
                core_recv.at[k],
                dom_id(peer),
            )

        def z1_copies(k):
            return (
                copy(
                    core_sum.at[k, rows_of((1 - s1) * 32, 32), :],
                    z1_in.at[k, 0],
                    z1_send.at[k, 0],
                    z1_recv.at[k, 0],
                    dom_id(za),
                ),
                copy(
                    core_sum.at[k, rows_of(64 + (1 - t1) * 32, 32), :],
                    z1_in.at[k, 1],
                    z1_send.at[k, 1],
                    z1_recv.at[k, 1],
                    dom_id(zb),
                ),
            )

        def z2_copies(k):
            return (
                copy(
                    z1_sum.at[k, 0, rows_of((1 - s2) * 16, 16), :],
                    z2_in.at[k, 0],
                    z2_send.at[k, 0],
                    z2_recv.at[k, 0],
                    dom_id(zb),
                ),
                copy(
                    z1_sum.at[k, 1, rows_of((1 - t2) * 16, 16), :],
                    z2_in.at[k, 1],
                    z2_send.at[k, 1],
                    z2_recv.at[k, 1],
                    dom_id(za),
                ),
            )

        row_1 = core * 128 + s1 * 32 + s2 * 16
        row_2 = core * 128 + 64 + t1 * 32 + t2 * 16

        def plane_copy(k, o):
            q = (p + o) % 16
            return copy(
                block.at[k, rows_of((q // 4) * 8, 8), pl.ds(pl.multiple_of((q % 4) * KQ, KQ), KQ)],
                plane_in.at[k, o],
                plane_send.at[k, o],
                plane_recv.at[k, o],
                plane_id(q),
            )

        my_tile = p // 4
        half = my_tile // 2
        own_row = row_1 + half * (row_2 - row_1) + (my_tile % 2) * 8
        own_lane = (p % 4) * KQ

        def own_tile(k):
            return (rows_of(own_row, 8), pl.ds(pl.multiple_of(k * KC + own_lane, KQ), KQ))

        def back_copy(k, o):
            q = (p + o) % 16
            return copy(
                back_out.at[k, q // 2],
                upd.at[own_tile(k)],
                back_send.at[k, o],
                back_recv.at[k, o],
                plane_id(q),
            )

        def back_wait(k, o):
            q = (p + 16 - o) % 16
            tile = q // 4
            row = row_1 + (tile // 2) * (row_2 - row_1) + (tile % 2) * 8
            dst = upd.at[rows_of(row, 8), pl.ds(pl.multiple_of(k * KC + (q % 4) * KQ, KQ), KQ)]
            copy(back_out.at[k, 0], dst, back_send.at[k, o], back_recv.at[k, o], plane_id(q)).wait_recv()

        def g2_copies(k):
            a = upd.at[rows_of(row_1, 16), pl.ds(k * KC, KC)]
            b = upd.at[rows_of(row_2, 16), pl.ds(k * KC, KC)]
            return (
                copy(a, a, g2_send.at[k, 0], g2_recv.at[k, 0], dom_id(zb)),
                copy(b, b, g2_send.at[k, 1], g2_recv.at[k, 1], dom_id(za)),
            )

        def g2_waits(k):
            a = upd.at[rows_of(core * 128 + s1 * 32 + (1 - s2) * 16, 16), pl.ds(k * KC, KC)]
            b = upd.at[rows_of(core * 128 + 64 + t1 * 32 + (1 - t2) * 16, 16), pl.ds(k * KC, KC)]
            copy(a, a, g2_send.at[k, 0], g2_recv.at[k, 0], dom_id(zb)).wait_recv()
            copy(b, b, g2_send.at[k, 1], g2_recv.at[k, 1], dom_id(za)).wait_recv()

        def g1_copies(k):
            a = upd.at[rows_of(core * 128 + s1 * 32, 32), pl.ds(k * KC, KC)]
            b = upd.at[rows_of(core * 128 + 64 + t1 * 32, 32), pl.ds(k * KC, KC)]
            return (
                copy(a, a, g1_send.at[k, 0], g1_recv.at[k, 0], dom_id(za)),
                copy(b, b, g1_send.at[k, 1], g1_recv.at[k, 1], dom_id(zb)),
            )

        def g1_waits(k):
            a = upd.at[rows_of(core * 128 + (1 - s1) * 32, 32), pl.ds(k * KC, KC)]
            b = upd.at[rows_of(core * 128 + 64 + (1 - t1) * 32, 32), pl.ds(k * KC, KC)]
            copy(a, a, g1_send.at[k, 0], g1_recv.at[k, 0], dom_id(za)).wait_recv()
            copy(b, b, g1_send.at[k, 1], g1_recv.at[k, 1], dom_id(zb)).wait_recv()

        def gc_copy(k):
            a = upd.at[rows_of(core * 128, 128), pl.ds(k * KC, KC)]
            return copy(a, a, gc_send.at[k], gc_recv.at[k], dom_id(peer))

        def gc_wait(k):
            a = upd.at[rows_of((1 - core) * 128, 128), pl.ds(k * KC, KC)]
            copy(a, a, gc_send.at[k], gc_recv.at[k], dom_id(peer)).wait_recv()

        fac_x = power(lev_x)
        fac_v = power(lev_v)

        def stage_project(k):
            part[:, cols_of(k)] = dot3(red_h[...], red_l[...], bx_h[:, cols_of(k)], bx_l[:, cols_of(k)], NN)
            core_copy(k).start()

        def stage_core(k):
            core_copy(k).wait_recv()
            core_sum[k] = part[rows_of(core * 128, 128), cols_of(k)] + core_in[k]
            for cp in z1_copies(k):
                cp.start()

        def stage_z1(k):
            for cp in z1_copies(k):
                cp.wait_recv()
            z1_sum[k, 0] = core_sum[k, rows_of(s1 * 32, 32), :] + z1_in[k, 0]
            z1_sum[k, 1] = core_sum[k, rows_of(64 + t1 * 32, 32), :] + z1_in[k, 1]
            for cp in z2_copies(k):
                cp.start()

        def stage_z2(k):
            for cp in z2_copies(k):
                cp.wait_recv()
            for h, (keep, base) in enumerate(((s2, row_1), (t2, row_2))):
                total = z1_sum[k, h, rows_of(keep * 16, 16), :] + z2_in[k, h]
                mode_x = (lax.broadcasted_iota(jnp.int32, (16, KC), 1) + k * KC).astype(F32)
                mode_v = (lax.broadcasted_iota(jnp.int32, (16, KC), 0) + base).astype(F32)
                bend_x = mode_x * fac_x * (1.0 / MX)
                bend_v = mode_v * fac_v * (1.0 / MV)
                weight = 1.0 / ((1.0 + bend_x * bend_x) * (1.0 + bend_v * bend_v))
                scale_x = jnp.where(mode_x == 0.0, 1.0 / NX, 2.0 / NX).astype(F32)
                scale_v = jnp.where(mode_v == 0.0, 1.0 / NV, 2.0 / NV).astype(F32)
                block[k, h * 16 : (h + 1) * 16, :] = total * (weight * (scale_x * scale_v))
            for o in range(1, 16):
                plane_copy(k, o).start()

        def stage_plane(k):
            mine = block[k, rows_of((p // 4) * 8, 8), pl.ds(pl.multiple_of((p % 4) * KQ, KQ), KQ)]
            plane_in[k, 0] = mine
            for o in range(1, 16):
                plane_copy(k, o).wait_recv()
            if k == 0:
                for o in range(1, 8):
                    copy(
                        coef_own, coef_all.at[(c + 8 - o) % 8], coef_send.at[o], coef_recv.at[o], {"comp": c, "dom": d}
                    ).wait_recv()
            own = []
            for g in range(8):
                a = plane_in[k, (p + 16 - 2 * g) % 16]
                b = plane_in[k, (p + 16 - 2 * g - 1) % 16]
                own.append(a + b)
            total = jnp.zeros((8, KQ), F32)
            for g in range(8):
                total = total + coef_all[g][:, 0:1] * own[g]
            for g in range(8):
                back_out[k, g] = total - own[g]
            upd[own_tile(k)] = back_out[k, c]
            for o in range(1, 16):
                back_copy(k, o).start()

        def stage_back(k):
            for o in range(1, 16):
                back_wait(k, o)
            for cp in g2_copies(k):
                cp.start()

        def stage_g2(k):
            g2_waits(k)
            for cp in g1_copies(k):
                cp.start()

        def stage_g1(k):
            g1_waits(k)
            gc_copy(k).start()

        def stage_gc(k):
            gc_wait(k)
            u_hi, u_lo = split(upd[:, cols_of(k)])
            term = dot3(u_hi, u_lo, bx_h[:, cols_of(k)], bx_l[:, cols_of(k)], NT)
            if k == 0:
                corr[...] = term
            else:
                corr[...] += term

        stages = (stage_project, stage_core, stage_z1, stage_z2, stage_plane, stage_back, stage_g2, stage_g1, stage_gc)
        for tick in range(NCH + len(stages) - 1):
            for s in reversed(range(len(stages))):
                if 0 <= tick - s < NCH:
                    with scope('G_%d_%s' % (tick - s, stages[s].__name__)):
                        stages[s](tick - s)
            if tick == 1:
                with scope("G_bt"):
                    lax.fori_loop(0, NV // 64, cell_rows, 0)

        with scope("H_expand"):
            for half in range(2):
                c_hi, c_lo = split(corr[:, half * 256 : (half + 1) * 256])
                for kt in range(TILES // 2):
                    rows = slice(kt * 256, (kt + 1) * 256)
                    cut = slice(PAD + kt * 256, PAD + (kt + 1) * 256)
                    add = dot3(bt_h[rows, :], bt_l[rows, :], c_hi, c_lo, NN)
                    fa[2 * half, cut, :] += add[:, :LANES]
                    fa[2 * half + 1, cut, :] += add[:, LANES:]
            edges(fa)

        with scope('H_sent'):
            for o in range(1, 8):
                coef_copy(o).wait_send()
            for k in range(NCH):
                core_copy(k).wait_send()
                gc_copy(k).wait_send()
                for group in (z1_copies(k), z2_copies(k), g2_copies(k), g1_copies(k)):
                    for cp in group:
                        cp.wait_send()
                for o in range(1, 16):
                    plane_copy(k, o).wait_send()
                    back_copy(k, o).wait_send()


    def two_steps(i, _):
        @pl.when(i == PRE // 2)
        def _():
            correct()

        with scope("E_step"):
            for src, dst, s in ((fa, fb, 2 * i), (fb, fa, 2 * i + 1)):
                on = (lev_x + (PRE - 3) > s) | (s >= PRE)
                step(src, dst, jnp.where(on, 1.0, 0.0).astype(F32))
        return 0

    lax.fori_loop(0, (PRE + POST) // 2, two_steps, 0)

    def store(t):
        return pltpu.make_async_copy(
            cells.at[t, pl.ds(LEAD, ROWS), :],
            out_ref.at[0, :, pl.ds(pl.multiple_of(t * LANES, LANES), LANES)],
            out_sem.at[t],
        )

    with scope("J_turn"):
        low, high = LEAD // SPAN, (LEAD + ROWS) // SPAN

        def turn_out(t, _):
            for q in range(SPAN):
                tile = fa[q, pl.ds(pl.multiple_of(PAD + t * LANES, 8), LANES), :].T
                cells[t, pl.ds(LEAD + q, high - low, stride=SPAN), :] = tile[low:high]
            store(t).start()
            return 0

        lax.fori_loop(0, TILES, turn_out, 0, unroll=4)

    with scope('K_tail'):
        for t in range(TILES):
            store(t).wait()


def body(densities, levels, coeffs):
    dma = pltpu.SemaphoreType.DMA
    vmem = pltpu.VMEM
    return pl.pallas_call(
        kernel,
        out_shape=jax.ShapeDtypeStruct((1, ROWS, NV), F32),
        in_specs=[
            pl.BlockSpec(memory_space=pltpu.SMEM),
            pl.BlockSpec(memory_space=pltpu.SMEM),
            pl.BlockSpec(memory_space=pl.ANY),
        ],
        out_specs=pl.BlockSpec(memory_space=pl.ANY),
        scratch_shapes=[
            vmem((TILES, WIDE, LANES), F32),
            vmem((SPAN, NV + 2 * PAD, LANES), F32),
            vmem((SPAN, NV + 2 * PAD, LANES), F32),
            vmem((WIDE, MX), BF16),
            vmem((WIDE, MX), BF16),
            vmem((MV, NV), BF16),
            vmem((MV, NV), BF16),
            vmem((NV, MV), BF16),
            vmem((NV, MV), BF16),
            vmem((MV, WIDE), BF16),
            vmem((MV, WIDE), BF16),
            vmem((MV, MX), F32),
            vmem((NCH, 128, KC), F32),
            vmem((NCH, 128, KC), F32),
            vmem((NCH, 2, 32, KC), F32),
            vmem((NCH, 2, 32, KC), F32),
            vmem((NCH, 2, 16, KC), F32),
            vmem((NCH, 32, KC), F32),
            vmem((NCH, 16, 8, KQ), F32),
            vmem((NCH, 8, 8, KQ), F32),
            vmem((MV, MX), F32),
            vmem((MV, WIDE), F32),
            vmem((8, LANES), F32),
            vmem((8, 8, LANES), F32),
            dma((TILES,)),
            dma((TILES,)),
            dma((2,)),
            dma((2,)),
            dma((8,)),
            dma((8,)),
            dma((NCH,)),
            dma((NCH,)),
            dma((NCH, 2)),
            dma((NCH, 2)),
            dma((NCH, 2)),
            dma((NCH, 2)),
            dma((NCH, 16)),
            dma((NCH, 16)),
            dma((NCH, 16)),
            dma((NCH, 16)),
            dma((NCH, 2)),
            dma((NCH, 2)),
            dma((NCH, 2)),
            dma((NCH, 2)),
            dma((NCH,)),
            dma((NCH,)),
        ],
        compiler_params=pltpu.CompilerParams(
            collective_id=0, has_side_effects=True, vmem_limit_bytes=60 * 1024 * 1024
        ),
        name="window",
    )(levels, coeffs, densities)


def solution(mesh):
    placed = (P("comp", "dom", None), P("comp", None), P("comp"))
    return jax.shard_map(
        body, mesh=mesh, in_specs=placed, out_specs=P("comp", "dom", None), check_vma=False
    )
```

time: 88.9 us -> 77.8 us (0.88)
  Pallas kernels: 84.2 us -> 73.1 us
    pallas_call x1, Pallas kernels: 84.2 us -> 73.1 us  [body(): pl.pallas_call(kernel, out_shape=jax.ShapeDtypeStruct((1, ROWS, NV), F32)...]
where the time goes in v2:
time: 77.8 us; the launch traced here: 77.6 us
  Pallas kernels  73.1 us (94%)
  local copies, waits for them, and re-layouts  3.91 us (5%)
    pallas_call x1, Pallas kernels, body(): pl.pallas_call(kernel, out_shape=jax.ShapeDtypeStruct((1, ROWS, NV), F32)...  73.1 us
    unnamed x1, local copies, waits for them, and re-layouts  3.91 us

profile of v2, /device:TPU:1, one launch (start us, length us, event | category | flops | bytes accessed | tf_op | source)
XLA Modules:
  0.0 77.6 jit_solution(15633888221507015681)
XLA Ops:
  0.7 73.1 %window.1 = f32[1,384,2048]{2,1,0:T(8,128)} custom-call(s32[1,2]{1,0:T(1,128)} %lev_ref.1, s32[1]{0:T(128)S(6)} %copy.5.coef_ref, f32[1,384,2048]{2,1,0:T(8,128)} %dens_ref.1), custom_call_target="tpu_custom_call" | custom-call | tf_op jit(solution)/shard_map/window/pallas_call | solution.py:627
  73.7 3.9 %copy.6 = f32[1,384,2048]{2,1,0:T(8,128)} copy(f32[1,384,2048]{2,1,0:T(8,128)} %window.1) | data formatting | bytes 6291456

commit v3 on v2

--- a/solution.py
+++ b/solution.py
@@ -22,7 +22,8 @@
 LEAD = 64
 WIDE = SPAN * LANES
 PAD = 8
-NCH = 2
+EARLY = 3
+NCH = 4
 KC = MX // NCH
 KQ = KC // 4
 MESH = pl.DeviceIdType.MESH
@@ -229,7 +230,6 @@
 
     with scope("A_bv"):
         lax.fori_loop(0, MV // 16, mode_rows, 0)
-        fill_space_basis(0)
 
     with scope('B_barrier'):
         for t in range(TILES):
@@ -269,7 +269,7 @@
         coef_copy(o).start()
 
     with scope("C_bx"):
-        for k in range(1, NCH):
+        for k in range(EARLY):
             fill_space_basis(k)
 
     def edges(dst):
@@ -550,14 +550,22 @@
                 corr[...] += term
 
         stages = (stage_project, stage_core, stage_z1, stage_z2, stage_plane, stage_back, stage_g2, stage_g1, stage_gc)
-        for tick in range(NCH + len(stages) - 1):
-            for s in reversed(range(len(stages))):
-                if 0 <= tick - s < NCH:
-                    with scope('G_%d_%s' % (tick - s, stages[s].__name__)):
-                        stages[s](tick - s)
-            if tick == 1:
-                with scope("G_bt"):
-                    lax.fori_loop(0, NV // 64, cell_rows, 0)
+        def run_stage(n, k):
+            with scope("G_%d_%s" % (k, stages[n].__name__)):
+                stages[n](k)
+
+        for k in range(NCH):
+            if k >= EARLY:
+                fill_space_basis(k)
+            run_stage(0, k)
+            if k > 0:
+                run_stage(1, k - 1)
+        run_stage(1, NCH - 1)
+        with scope("G_bt"):
+            lax.fori_loop(0, NV // 64, cell_rows, 0)
+        for n in range(2, len(stages)):
+            for k in range(NCH):
+                run_stage(n, k)
 
         with scope("H_expand"):
             for half in range(2):
@@ -597,13 +605,6 @@
 
     lax.fori_loop(0, (PRE + POST) // 2, two_steps, 0)
 
-    def store(t):
-        return pltpu.make_async_copy(
-            cells.at[t, pl.ds(LEAD, ROWS), :],
-            out_ref.at[0, :, pl.ds(pl.multiple_of(t * LANES, LANES), LANES)],
-            out_sem.at[t],
-        )
-
     with scope("J_turn"):
         low, high = LEAD // SPAN, (LEAD + ROWS) // SPAN
 
@@ -611,14 +612,10 @@
             for q in range(SPAN):
                 tile = fa[q, pl.ds(pl.multiple_of(PAD + t * LANES, 8), LANES), :].T
                 cells[t, pl.ds(LEAD + q, high - low, stride=SPAN), :] = tile[low:high]
-            store(t).start()
+            out_ref[0, :, pl.ds(pl.multiple_of(t * LANES, LANES), LANES)] = cells[t, LEAD : LEAD + ROWS, :]
             return 0
 
         lax.fori_loop(0, TILES, turn_out, 0, unroll=4)
-
-    with scope('K_tail'):
-        for t in range(TILES):
-            store(t).wait()
 
 
 def body(densities, levels, coeffs):
@@ -626,13 +623,13 @@
     vmem = pltpu.VMEM
     return pl.pallas_call(
         kernel,
-        out_shape=jax.ShapeDtypeStruct((1, ROWS, NV), F32),
+        out_shape=pltpu.VMEM((1, ROWS, NV), F32),
         in_specs=[
             pl.BlockSpec(memory_space=pltpu.SMEM),
             pl.BlockSpec(memory_space=pltpu.SMEM),
             pl.BlockSpec(memory_space=pl.ANY),
         ],
-        out_specs=pl.BlockSpec(memory_space=pl.ANY),
+        out_specs=pl.BlockSpec(memory_space=pltpu.VMEM),
         scratch_shapes=[
             vmem((TILES, WIDE, LANES), F32),
             vmem((SPAN, NV + 2 * PAD, LANES), F32),

time: 77.8 us -> 69.5 us (0.89)
  Pallas kernels: 73.1 us -> 67.1 us
  local copies, waits for them, and re-layouts: 3.91 us -> 1.67 us
    pallas_call x1, Pallas kernels: 73.1 us -> 67.1 us  [body(): pl.pallas_call(kernel, out_shape=pltpu.VMEM((1, ROWS, NV), F32), in_specs...]
    unnamed x1, local copies, waits for them, and re-layouts: 3.91 us -> 1.67 us
where the time goes in v3:
time: 69.5 us; the launch traced here: 69.4 us
  Pallas kernels  67.1 us (97%)
  local copies, waits for them, and re-layouts  1.67 us (2%)
    pallas_call x1, Pallas kernels, body(): pl.pallas_call(kernel, out_shape=pltpu.VMEM((1, ROWS, NV), F32), in_specs...  67.1 us
    unnamed x1, local copies, waits for them, and re-layouts  1.67 us

profile of v3, /device:TPU:1, one launch (start us, length us, event | category | flops | bytes accessed | tf_op | source)
XLA Modules:
  0.0 69.4 jit_solution(3612705778547575205)
XLA Ops:
  0.7 67.1 %window.1 = f32[1,384,2048]{2,1,0:T(8,128)S(1)} custom-call(s32[1,2]{1,0:T(1,128)} %lev_ref.1, s32[1]{0:T(128)S(6)} %copy.6.coef_ref, f32[1,384,2048]{2,1,0:T(8,128)} %dens_ref.1), custom_call_target="tpu_custom_call" | custom-call | tf_op jit(solution)/shard_map/window/pallas_call | solution.py:624
  67.8 1.7 %copy.5 = f32[1,384,2048]{2,1,0:T(8,128)} copy(f32[1,384,2048]{2,1,0:T(8,128)S(1)} %window.1) | data formatting | bytes 6291456

commit v4 on v3

--- a/solution.py
+++ b/solution.py
@@ -19,9 +19,11 @@
 TILES = NV // LANES
 HALO = 16
 SPAN = 4
-LEAD = 64
+LEAD = 32
+USED = 112
 WIDE = SPAN * LANES
 PAD = 8
+PLAIN = 2
 EARLY = 3
 NCH = 4
 KC = MX // NCH
@@ -194,25 +196,20 @@
             bv_l[pl.ds(r0, 16), t * LANES : (t + 1) * LANES] = lo
         return 0
 
-    def cell_rows(i, _):
-        for b in range(4):
-            r0 = pl.multiple_of(i * 64 + b * 16, 16)
-            angle = np.float32(np.pi) * ((row16 + r0).astype(F32) + 0.5)
-            for t in range(MV // LANES):
-                mode = (lane + t * LANES).astype(F32)
-                phase = (angle * mode) * np.float32(1.0 / NV)
-                hi, lo = split(cosine(phase))
-                bt_h[pl.ds(r0, 16), t * LANES : (t + 1) * LANES] = hi
-                bt_l[pl.ds(r0, 16), t * LANES : (t + 1) * LANES] = lo
+    def turn_basis(t, _):
+        cols = pl.ds(pl.multiple_of(t * LANES, LANES), LANES)
+        bt_h[cols, :] = bv_h[:, cols].T
+        bt_l[cols, :] = bv_l[:, cols].T
         return 0
 
     def space_basis(k, i):
-        local = (row16 + (i % 8) * 16) * SPAN + i // 8 - LEAD
+        plane, first = i // (USED // 16), (i % (USED // 16)) * 16
+        local = (row16 + first) * SPAN + plane - LEAD
         cell = local + d * ROWS
         cell = jnp.where(cell < 0, cell + NX, cell)
         cell = jnp.where(cell >= NX, cell - NX, cell)
         angle = np.float32(np.pi) * (cell.astype(F32) + 0.5)
-        r0 = pl.multiple_of(i * 16, 16)
+        r0 = pl.multiple_of(plane * LANES + first, 16)
         for t in range(k * KC // LANES, (k + 1) * KC // LANES):
             mode = (lane + t * LANES).astype(F32)
             phase = (angle * mode) * np.float32(1.0 / NX)
@@ -226,7 +223,12 @@
             space_basis(k, 2 * i + 1)
             return 0
 
-        lax.fori_loop(0, WIDE // 32, run, 0)
+        lax.fori_loop(0, SPAN * USED // 32, run, 0)
+        for q in range(SPAN):
+            rest = slice(q * LANES + USED, (q + 1) * LANES)
+            cols = slice(k * KC, (k + 1) * KC)
+            bx_h[rest, cols] = jnp.zeros((LANES - USED, KC), BF16)
+            bx_l[rest, cols] = jnp.zeros((LANES - USED, KC), BF16)
 
     with scope("A_bv"):
         lax.fori_loop(0, MV // 16, mode_rows, 0)
@@ -280,10 +282,11 @@
     row_v = lax.broadcasted_iota(jnp.int32, (16, LANES), 0)
     offsets = (2.0 * row_v.astype(F32) + 1.0) / NV - 1.0
 
-    def step(src, dst, active):
-        rate = active * diffusion
-        keep = 1.0 - 2.0 * rate
-        pace = active * courant
+    def step(src, dst, active, scale, unit):
+        share = 1.0 / diffusion if unit else scale
+        rate = active * diffusion * share
+        keep = share - 2.0 * rate
+        pace = active * courant * share
 
         def part_of(first, upper):
             r = first + PAD
@@ -297,7 +300,9 @@
                 shifted = f[1:] + [pltpu.roll(f[0], LANES - 1, 1)]
             for q in range(SPAN):
                 pair = src[q, r - 1 : r + 15, :] + src[q, r + 1 : r + 17, :]
-                dst[q, r : r + 16, :] = al * f[q] + be * shifted[q] + rate * pair
+                if not unit:
+                    pair = rate * pair
+                dst[q, r : r + 16, :] = al * f[q] + be * shifted[q] + pair
 
         for first in range(0, NV, 16):
             part_of(first, first >= NV // 2)
@@ -562,10 +567,16 @@
                 run_stage(1, k - 1)
         run_stage(1, NCH - 1)
         with scope("G_bt"):
-            lax.fori_loop(0, NV // 64, cell_rows, 0)
-        for n in range(2, len(stages)):
+            lax.fori_loop(0, TILES, turn_basis, 0, unroll=4)
+        for n in range(2, len(stages) - 2):
             for k in range(NCH):
                 run_stage(n, k)
+        for k in range(NCH):
+            run_stage(len(stages) - 2, k)
+            if k > 1:
+                run_stage(len(stages) - 1, k - 2)
+        for k in range(NCH - 2, NCH):
+            run_stage(len(stages) - 1, k)
 
         with scope("H_expand"):
             for half in range(2):
@@ -600,10 +611,19 @@
         with scope("E_step"):
             for src, dst, s in ((fa, fb, 2 * i), (fb, fa, 2 * i + 1)):
                 on = (lev_x + (PRE - 3) > s) | (s >= PRE)
-                step(src, dst, jnp.where(on, 1.0, 0.0).astype(F32))
+                scale = jnp.where(s == 2 * PLAIN, rescale, 1.0) if dst is fb else 1.0
+                step(src, dst, jnp.where(on, 1.0, 0.0).astype(F32), scale, False)
         return 0
 
-    lax.fori_loop(0, (PRE + POST) // 2, two_steps, 0)
+    def two_plain(i, _):
+        with scope("E_step"):
+            step(fa, fb, 1.0, 1.0, True)
+            step(fb, fa, 1.0, 1.0, True)
+        return 0
+
+    rescale = (diffusion * diffusion) * (diffusion * diffusion)
+    lax.fori_loop(0, PLAIN, two_plain, 0)
+    lax.fori_loop(PLAIN, (PRE + POST) // 2, two_steps, 0)
 
     with scope("J_turn"):
         low, high = LEAD // SPAN, (LEAD + ROWS) // SPAN

time: 69.5 us -> 69 us (level)
  no operation moved by 1% of the time
where the time goes in v4:
time: 69 us; the launch traced here: 68.8 us
  Pallas kernels  66.5 us (96%)
  local copies, waits for them, and re-layouts  1.67 us (2%)
    pallas_call x1, Pallas kernels, body(): pl.pallas_call(kernel, out_shape=pltpu.VMEM((1, ROWS, NV), F32), in_specs...  66.5 us
    unnamed x1, local copies, waits for them, and re-layouts  1.67 us

profile of v4, /device:TPU:1, one launch (start us, length us, event | category | flops | bytes accessed | tf_op | source)
XLA Modules:
  0.0 68.8 jit_solution(16974300755187550880)
XLA Ops:
  0.7 66.5 %window.1 = f32[1,384,2048]{2,1,0:T(8,128)S(1)} custom-call(s32[1,2]{1,0:T(1,128)} %lev_ref.1, s32[1]{0:T(128)S(6)} %copy.6.coef_ref, f32[1,384,2048]{2,1,0:T(8,128)} %dens_ref.1), custom_call_target="tpu_custom_call" | custom-call | tf_op jit(solution)/shard_map/window/pallas_call | solution.py:644
  67.2 1.7 %copy.5 = f32[1,384,2048]{2,1,0:T(8,128)} copy(f32[1,384,2048]{2,1,0:T(8,128)S(1)} %window.1) | data formatting | bytes 6291456

commit v5 on v4

--- a/solution.py
+++ b/solution.py
@@ -565,9 +565,9 @@
             run_stage(0, k)
             if k > 0:
                 run_stage(1, k - 1)
-        run_stage(1, NCH - 1)
         with scope("G_bt"):
             lax.fori_loop(0, TILES, turn_basis, 0, unroll=4)
+        run_stage(1, NCH - 1)
         for n in range(2, len(stages) - 2):
             for k in range(NCH):
                 run_stage(n, k)

time: 69 us -> 69.1 us (level)
  no operation moved by 1% of the time
where the time goes in v5:
time: 69.1 us; the launch traced here: 69 us
  Pallas kernels  66.6 us (96%)
  local copies, waits for them, and re-layouts  1.67 us (2%)
    pallas_call x1, Pallas kernels, body(): pl.pallas_call(kernel, out_shape=pltpu.VMEM((1, ROWS, NV), F32), in_specs...  66.6 us
    unnamed x1, local copies, waits for them, and re-layouts  1.67 us

profile of v5, /device:TPU:1, one launch (start us, length us, event | category | flops | bytes accessed | tf_op | source)
XLA Modules:
  0.0 69.0 jit_solution(12870033732992913708)
XLA Ops:
  0.7 66.6 %window.1 = f32[1,384,2048]{2,1,0:T(8,128)S(1)} custom-call(s32[1,2]{1,0:T(1,128)} %lev_ref.1, s32[1]{0:T(128)S(6)} %copy.6.coef_ref, f32[1,384,2048]{2,1,0:T(8,128)} %dens_ref.1), custom_call_target="tpu_custom_call" | custom-call | tf_op jit(solution)/shard_map/window/pallas_call | solution.py:644
  67.3 1.7 %copy.5 = f32[1,384,2048]{2,1,0:T(8,128)} copy(f32[1,384,2048]{2,1,0:T(8,128)S(1)} %window.1) | data formatting | bytes 6291456
